TPU v7x, 32 devices: a whole 2x2x4 slice. The times are simulated.
32 devices in a mesh: cp: 8 (over z, x), tp: 4 (over y, core).
Axes of the slice: x: 2, y: 2, z: 4, core: 2. Of those that a mesh axis runs over, the one named last changes fastest.
Arguments:
- queries: bfloat16 [1536, 2048], P('cp', 'tp'), may hold values from -128 to 128
- keys: bfloat16 [1536, 256], P('cp'), may hold values from -6 to 6
- values: bfloat16 [1536, 256], P('cp'), may hold values from -6 to 6
- positions: int32 [1536], replicated, may hold values from 0 to 1535, as said below
- out_weight: bfloat16 [2048, 8192], P('tp'), may hold values from -0.125 to 0.125
Outputs:
- mixed: bfloat16 [1536, 8192], P(('cp', 'tp'))
Inputs may be any that keep to these rules, and one draw needn't show every extreme that they name: positions is a permutation of 0 to 1535. The tokens stored at indices d * 192 to (d + 1) * 192 - 1 form two runs of 96 consecutive positions, the first starting at b * 96 and the second at (15 - b) * 96 for some b, each b used by one d.
All inputs are finite; a program needn't handle non-finite values.
Results may differ from a plain program's by a relative error of at most 0.013.
Values may be sent and summed in bfloat16 or wider, within the bound.
A program may use at most 128 MiB of HBM per device.

v0:
```python
import jax
import jax.numpy as jnp
from jax import lax
from jax.sharding import PartitionSpec as P

HEAD = 128
GROUP = 8


def shards(queries, keys, values, positions, out_weight):
    tok_rows = queries.shape[0]
    head_count = queries.shape[1] // HEAD
    score_scale = HEAD ** (-0.5)
    kv_group = lax.axis_index("tp") * head_count // GROUP
    own_keys = lax.dynamic_slice_in_dim(keys, kv_group * HEAD, HEAD, 1)
    own_values = lax.dynamic_slice_in_dim(values, kv_group * HEAD, HEAD, 1)
    query_pos = lax.dynamic_slice_in_dim(positions, lax.axis_index("cp") * tok_rows, tok_rows, 0)
    local_queries = queries.reshape(tok_rows, head_count, HEAD)
    run_max = jnp.full((tok_rows, head_count), -1e30, jnp.float32)
    arrived_keys = lax.all_gather(own_keys, "cp", axis=0, tiled=True)
    arrived_values = lax.all_gather(own_values, "cp", axis=0, tiled=True)
    allowed = (positions[None, :] <= query_pos[:, None])[:, None, :]
    scores = (
        jnp.einsum("qhd,kd->qhk", local_queries, arrived_keys, preferred_element_type=jnp.float32)
        * score_scale
    )
    scores = jnp.where(allowed, scores, -1e30)
    new_max = jnp.maximum(run_max, jnp.max(scores, axis=-1))
    weights = jnp.where(allowed, jnp.exp(scores - new_max[:, :, None]), 0.0)
    run_sum = jnp.sum(weights, axis=-1)
    run_out = jnp.einsum(
        "qhk,kd->qhd",
        weights.astype(jnp.bfloat16),
        arrived_values,
        preferred_element_type=jnp.float32,
    )
    final_state = (new_max, run_sum, run_out)
    run_max, run_sum, run_out = final_state
    attended = (
        (run_out / run_sum[:, :, None]).astype(jnp.bfloat16).reshape(tok_rows, head_count * HEAD)
    )
    return lax.psum_scatter(
        jnp.dot(attended, out_weight, preferred_element_type=jnp.float32).astype(jnp.bfloat16),
        "tp",
        scatter_dimension=0,
        tiled=True,
    )


def solution(mesh):
    in_specs = (P("cp", "tp"), P("cp", None), P("cp", None), P(), P("tp", None))
    out_specs = P(("cp", "tp"), None)
    return jax.shard_map(shards, mesh=mesh, in_specs=in_specs, out_specs=out_specs, check_vma=False)
```

profile of v0, /device:TPU:0, one launch (start us, length us, event | category | flops | bytes accessed | tf_op | source)
XLA Modules:
  0.0 127.3 jit_solution(13655687156293303523)
XLA Ops:
  6.5 0.0 copy-start
  6.5 0.0 copy-start.1
  6.5 0.0 reduce-scatter.2.cloned.1.call-start
  6.5 0.8 constant_dynamic-slice_fusion.1
  7.4 32.8 %all_gather.6 = bf16[1536,128]{1,0:T(8,128)(2,1)S(1)} all-gather(bf16[192,128]{1,0:T(8,128)(2,1)S(1)} %constant_dynamic-slice_fusion.1), channel_id=1, replica_groups=mesh['cp'=8,'tp'=4] {'cp'}, dimensions={0}, use_global_device_ids=true | all-gather | bytes 442368 | tf_op jit(solution)/shard_map/all_gather | solution.py:20
  40.2 0.8 dynamic_slice.9
  40.9 0.9 broadcast_compare_fusion
  41.9 0.0 copy-done
  41.9 1.1 fusion
  43.0 0.0 copy-done.1
  43.0 31.0 %all_gather.7 = bf16[1536,128]{1,0:T(8,128)(2,1)S(1)} all-gather(bf16[192,128]{1,0:T(8,128)(2,1)S(1)} %constant_dynamic-slice_fusion), channel_id=1, replica_groups=mesh['cp'=8,'tp'=4] {'cp'}, dimensions={0}, use_global_device_ids=true | all-gather | bytes 442368 | tf_op jit(solution)/shard_map/all_gather | solution.py:21
  74.0 0.0 slice-start
  74.0 1.5 %fusion.1 = f32[192,4]{0,1:T(4,128)S(1)} fusion(f32[1536,192,4]{0,1,2:T(8,128)S(1)} %get-tuple-element.6, f32[192,4]{0,1:T(4,128)S(1)} %broadcast_maximum_fusion, pred[192,1536]{1,0:T(8,128)(4,1)S(1)} %broadcast_compare_fusion), kind=kLoop, calls=%fused_computation.4 | loop fusion | flops 5897472 | bytes 5019648 | tf_op jit(solution)/shard_map/reduce_sum | solution.py:30
  75.5 0.0 slice-start.1
  75.5 1.4 %fusion.12 = bf16[4,24,8,128]{3,2,1,0:T(8,128)(2,1)S(1)} fusion(f32[1536,192,4]{0,1,2:T(8,128)S(1)} %get-tuple-element.6, f32[192,4]{0,1:T(4,128)S(1)} %broadcast_maximum_fusion, pred[192,1536]{1,0:T(8,128)(4,1)S(1)} %broadcast_compare_fusion, bf16[1536,128]{1,0:T(8,128)(2,1)S(1)} %all_gather.7, f32[192,4]{0,1:T(4,128)S(1)} %fusion.1), kind=kOutput, calls=%fused_computation.10 | convolution fusion | flops 308084736 | bytes 5609472 | tf_op jit(solution)/shard_map/qhk,kd->qhd/dot_general | solution.py:31
  76.9 0.0 slice-done
  76.9 0.9 slice-done.1
  77.8 3.5 %convolution_convert_fusion = bf16[192,8192]{1,0:T(8,128)(2,1)} fusion(bf16[512,8192]{1,0:T(8,128)(2,1)S(1)} %bitcast.41, bf16[4,24,8,128]{3,2,1,0:T(8,128)(2,1)S(1)} %fusion.12), kind=kOutput, calls=%fused_computation | convolution fusion | flops 1612185600 | bytes 11730944 | tf_op jit(solution)/shard_map/dot_general | solution.py:43
  81.3 0.0 reduce-scatter.2.cloned.1.call-update
  81.3 39.2 %reduce-scatter.2.cloned.1.call-done = bf16[48,8192]{1,0:T(8,128)(2,1)} async-done(((bf16[192,8192]{1,0:T(8,128)(2,1)}), bf16[48,8192]{1,0:T(8,128)(2,1)}) %reduce-scatter.2.cloned.1.call-update) | async-done | bytes 786448 | tf_op jit(solution)/shard_map/reduce_scatter | solution.py:42
  (3 shorter events, 0.0 us)
Async XLA Ops:
  6.5 35.3 %copy-start = (bf16[192,512]{1,0:T(8,128)(2,1)S(1)}, bf16[192,512]{1,0:T(8,128)(2,1)}, u32[]{:S(2)}) copy-start(bf16[192,512]{1,0:T(8,128)(2,1)} %param.5) | copy-start | bytes 589828
  6.5 36.4 %copy-start.1 = (bf16[192,256]{1,0:T(8,128)(2,1)S(1)}, bf16[192,256]{1,0:T(8,128)(2,1)}, u32[]{:S(2)}) copy-start(bf16[192,256]{1,0:T(8,128)(2,1)} %param.7) | copy-start | bytes 294916
  6.5 114.0 %reduce-scatter.2.cloned.1.call-start = ((), (), s32[]{:S(2)}) async-start(), calls=%async_computation.1 | async-start | bytes 3932160 | tf_op jit(solution)/shard_map/reduce_scatter | solution.py:42
  74.0 2.9 %slice-start = ((s8[8388608]{0:T(1024)(128)(4,1)}), s8[4194304]{0:T(1024)(128)(4,1)S(1)}, s32[]{:S(2)}) async-start(s8[8388608]{0:T(1024)(128)(4,1)} %bitcast.40), calls=%async_computation.2 | async-start | bytes 8388608
  75.5 2.4 %slice-start.1 = ((s8[8388608]{0:T(1024)(128)(4,1)}), s8[4194304]{0:T(1024)(128)(4,1)S(1)}, s32[]{:S(2)}) async-start(s8[8388608]{0:T(1024)(128)(4,1)} %bitcast.40), calls=%async_computation.3 | async-start | bytes 8388608
Sparse Core Ops, SparseCore 0:
  81.4 39.0 reduce-scatter.1
where the time goes:
time: 128 us; the launch traced here: 127 us
  blocking collectives  63.7 us (50%)
  waiting for transfers between devices  39.2 us (31%)
  between operations  13.4 us (10%)
  matrix products  5.98 us (5%)
  local copies, waits for them, and re-layouts  2.58 us (2%)
  other arithmetic  2.41 us (2%)
    reduce_scatter x1, waiting for transfers between devices, shards(): lax.psum_scatter(jnp.dot(attended, out_weight, preferred_element_type=jnp...  39.2 us
    all_gather x1, blocking collectives, shards(): arrived_keys = lax.all_gather(own_keys, 'cp', axis=0, tiled=True)  32.8 us
    all_gather x1, blocking collectives, shards(): arrived_values = lax.all_gather(own_values, 'cp', axis=0, tiled=True)  31 us
    dot_general x1, matrix products, shards(): jnp.dot(attended, out_weight, preferred_element_type=jnp.float32)  3.47 us
  transfers between devices with their start and end apart: 1, of which 1 were waited for; matrix products, arithmetic and copies ran while one was open for 0% of the time, Pallas kernels for 0%

commit v1 on v0

--- a/solution.py
+++ b/solution.py
@@ -17,8 +17,11 @@
     query_pos = lax.dynamic_slice_in_dim(positions, lax.axis_index("cp") * tok_rows, tok_rows, 0)
     local_queries = queries.reshape(tok_rows, head_count, HEAD)
     run_max = jnp.full((tok_rows, head_count), -1e30, jnp.float32)
-    arrived_keys = lax.all_gather(own_keys, "cp", axis=0, tiled=True)
-    arrived_values = lax.all_gather(own_values, "cp", axis=0, tiled=True)
+    arrived_keys, arrived_values = jnp.split(
+        lax.all_gather(jnp.concatenate([own_keys, own_values], axis=1), "cp", axis=0, tiled=True),
+        [own_keys.shape[1]],
+        axis=1,
+    )
     allowed = (positions[None, :] <= query_pos[:, None])[:, None, :]
     scores = (
         jnp.einsum("qhd,kd->qhk", local_queries, arrived_keys, preferred_element_type=jnp.float32)

time: 128 us -> 97.6 us (0.76)
  blocking collectives: 63.7 us -> 33.9 us
    all_gather x2 -> x1, blocking collectives: 63.7 us -> 33.9 us  [shards(): lax.all_gather(jnp.concatenate([own_keys, own_values], axis=1), 'cp', axi...]
where the time goes in v1:
time: 97.6 us; the launch traced here: 97.3 us
  waiting for transfers between devices  39 us (40%)
  blocking collectives  33.9 us (35%)
  between operations  13.4 us (14%)
  matrix products  6.07 us (6%)
  local copies, waits for them, and re-layouts  2.5 us (3%)
  other arithmetic  2.45 us (3%)
    reduce_scatter x1, waiting for transfers between devices, shards(): lax.psum_scatter(jnp.dot(attended, out_weight, preferred_element_type=jnp...  39 us
    all_gather x1, blocking collectives, shards(): lax.all_gather(jnp.concatenate([own_keys, own_values], axis=1), 'cp', axi...  33.9 us
    dot_general x1, matrix products, shards(): jnp.dot(attended, out_weight, preferred_element_type=jnp.float32)  3.47 us
  transfers between devices with their start and end apart: 1, of which 1 were waited for; matrix products, arithmetic and copies ran while one was open for 0% of the time, Pallas kernels for 0%

profile of v1, /device:TPU:0, one launch (start us, length us, event | category | flops | bytes accessed | tf_op | source)
XLA Modules:
  0.0 97.3 jit_solution(7139296323277881688)
XLA Ops:
  6.5 0.0 copy-start
  6.5 0.0 reduce-scatter.2.cloned.1.call-start
  6.5 0.8 dynamic_slice.9
  7.3 0.9 broadcast_compare_fusion
  8.3 0.8 constant_dynamic-slice_fusion
  9.1 33.9 %all_gather.3 = bf16[1536,256]{1,0:T(8,128)(2,1)S(1)} all-gather(bf16[192,256]{1,0:T(8,128)(2,1)S(1)} %pad_maximum_fusion), channel_id=1, replica_groups=mesh['cp'=8,'tp'=4] {'cp'}, dimensions={0}, use_global_device_ids=true | all-gather | bytes 884736 | tf_op jit(solution)/shard_map/all_gather | solution.py:21
  43.0 0.0 copy-done
  43.0 1.1 %fusion = (f32[192,4]{0,1:T(4,128)S(1)}, f32[1536,192,4]{0,1,2:T(8,128)S(1)}) fusion(pred[192,1536]{1,0:T(8,128)(4,1)S(1)} %broadcast_compare_fusion, bf16[1536,256]{1,0:T(8,128)(2,1)S(1)} %all_gather.3, bf16[192,512]{1,0:T(8,128)(2,1)S(1)} %copy-done), kind=kOutput, calls=%fused_computation.3 | convolution fusion | flops 305528064 | bytes 5606400 | tf_op jit(solution)/shard_map/qhd,kd->qhk/dot_general | solution.py:27
  44.1 0.0 slice-start
  44.1 1.5 %fusion.1 = f32[192,4]{0,1:T(4,128)S(1)} fusion(f32[1536,192,4]{0,1,2:T(8,128)S(1)} %get-tuple-element.6, f32[192,4]{0,1:T(4,128)S(1)} %broadcast_maximum_fusion, pred[192,1536]{1,0:T(8,128)(4,1)S(1)} %broadcast_compare_fusion), kind=kLoop, calls=%fused_computation.4 | loop fusion | flops 5897472 | bytes 5019648 | tf_op jit(solution)/shard_map/reduce_sum | solution.py:33
  45.6 0.0 slice-start.1
  45.7 1.5 %fusion.12 = bf16[4,24,8,128]{3,2,1,0:T(8,128)(2,1)S(1)} fusion(f32[1536,192,4]{0,1,2:T(8,128)S(1)} %get-tuple-element.6, f32[192,4]{0,1:T(4,128)S(1)} %broadcast_maximum_fusion, pred[192,1536]{1,0:T(8,128)(4,1)S(1)} %broadcast_compare_fusion, bf16[1536,256]{1,0:T(8,128)(2,1)S(1)} %all_gather.3, f32[192,4]{0,1:T(4,128)S(1)} %fusion.1), kind=kOutput, calls=%fused_computation.10 | convolution fusion | flops 308084736 | bytes 5611520 | tf_op jit(solution)/shard_map/qhk,kd->qhd/dot_general | solution.py:34
  47.1 0.0 slice-done
  47.2 0.8 slice-done.1
  48.0 3.5 %convolution_convert_fusion = bf16[192,8192]{1,0:T(8,128)(2,1)} fusion(bf16[512,8192]{1,0:T(8,128)(2,1)S(1)} %bitcast.41, bf16[4,24,8,128]{3,2,1,0:T(8,128)(2,1)S(1)} %fusion.12), kind=kOutput, calls=%fused_computation | convolution fusion | flops 1612185600 | bytes 11730944 | tf_op jit(solution)/shard_map/dot_general | solution.py:46
  51.5 0.0 reduce-scatter.2.cloned.1.call-update
  51.5 39.0 %reduce-scatter.2.cloned.1.call-done = bf16[48,8192]{1,0:T(8,128)(2,1)} async-done(((bf16[192,8192]{1,0:T(8,128)(2,1)}), bf16[48,8192]{1,0:T(8,128)(2,1)}) %reduce-scatter.2.cloned.1.call-update) | async-done | bytes 786448 | tf_op jit(solution)/shard_map/reduce_scatter | solution.py:45
  (3 shorter events, 0.0 us)
Async XLA Ops:
  6.5 36.5 %copy-start = (bf16[192,512]{1,0:T(8,128)(2,1)S(1)}, bf16[192,512]{1,0:T(8,128)(2,1)}, u32[]{:S(2)}) copy-start(bf16[192,512]{1,0:T(8,128)(2,1)} %param.5) | copy-start | bytes 589828
  6.5 84.0 %reduce-scatter.2.cloned.1.call-start = ((), (), s32[]{:S(2)}) async-start(), calls=%async_computation.1 | async-start | bytes 3932160 | tf_op jit(solution)/shard_map/reduce_scatter | solution.py:45
  44.1 3.0 %slice-start = ((s8[8388608]{0:T(1024)(128)(4,1)}), s8[4194304]{0:T(1024)(128)(4,1)S(1)}, s32[]{:S(2)}) async-start(s8[8388608]{0:T(1024)(128)(4,1)} %bitcast.40), calls=%async_computation.2 | async-start | bytes 8388608
  45.6 2.4 %slice-start.1 = ((s8[8388608]{0:T(1024)(128)(4,1)}), s8[4194304]{0:T(1024)(128)(4,1)S(1)}, s32[]{:S(2)}) async-start(s8[8388608]{0:T(1024)(128)(4,1)} %bitcast.40), calls=%async_computation.3 | async-start | bytes 8388608
Sparse Core Ops, SparseCore 0:
  51.6 38.8 reduce-scatter.1
